TPU v7x, 32 devices: a whole 2x2x4 slice. The times are simulated.
32 devices in a mesh: rep: 4 (over x, core), mx: 2 (over y), my: 4 (over z).
Axes of the slice: x: 2, y: 2, z: 4, core: 2. Of those that a mesh axis runs over, the one named last changes fastest.
Arguments:
- coefficients: bfloat16 [2, 384, 384, 384], P(None, 'mx', 'my'), may hold values from -7.5 to 7.5
- noise_field: bfloat16 [128, 2, 1536, 1536], P(('rep', 'mx'), None, 'my'), may hold values from -96 to 96
- mode_table: bfloat16 [384, 1536], replicated, may hold values from -0.3125 to 0.3125
Outputs:
- update: bfloat16 [2, 384, 384, 384], P(None, 'mx', 'my', 'rep')
All inputs are finite; a program needn't handle non-finite values.
Results may differ from a plain program's by a relative error of at most 0.008.
Values may be sent and summed in bfloat16 or wider, within the bound.
A program may use at most 384 MiB of HBM per device.

v0:
```python
import jax
import jax.numpy as jnp
from jax import lax
from jax.sharding import PartitionSpec as P

DAMPING = 0.25


def body(coefficients, noise_field, mode_table):
    rep_index = lax.axis_index("rep")
    col_index = lax.axis_index("my")
    rep_count = lax.axis_size("rep")
    row_count = lax.axis_size("mx")
    col_count = lax.axis_size("my")
    planes_dev = noise_field.shape[0]
    planes_rep = planes_dev * row_count
    planes_all = planes_rep * rep_count
    mode_count = mode_table.shape[0]
    point_count = mode_table.shape[1]
    slab_first = point_count // 2 - planes_all // 2
    row_block = mode_count // row_count
    col_block = mode_count // col_count
    point_block = point_count // col_count
    own_block = mode_count // rep_count
    slab_own = lax.dynamic_slice_in_dim(
        mode_table, slab_first + rep_index * planes_rep, planes_rep, 1
    )
    zmodes = jnp.einsum(
        "pabk,kz->zpba", coefficients, slab_own, preferred_element_type=jnp.float32
    ).astype(jnp.bfloat16)
    zmodes = zmodes.reshape(planes_rep, 2, col_block * row_block)
    spread = lax.all_to_all(zmodes, "mx", split_axis=0, concat_axis=2, tiled=True)
    grouped = spread.reshape(planes_dev, 2, row_count, col_block, row_block)
    tiled_table = mode_table.reshape(row_count, row_block, point_count)
    own_points = lax.dynamic_slice_in_dim(tiled_table, col_index * point_block, point_block, 2)
    block_part = jnp.einsum(
        "zpsal,slx->zpax",
        lax.all_gather(grouped, "my", axis=3, tiled=True),
        own_points,
        preferred_element_type=jnp.float32,
    ).astype(jnp.bfloat16)
    wave_field = jnp.einsum(
        "zpax,ay->zpxy", block_part, mode_table, preferred_element_type=jnp.float32
    )
    wave_real = wave_field[:, 0]
    wave_imag = wave_field[:, 1]
    density = wave_real * wave_real + wave_imag * wave_imag
    noise_wide = noise_field.astype(jnp.float32)
    drive_term = jnp.stack(
        [
            density * (wave_imag - DAMPING * wave_real) + noise_wide[:, 0],
            density * (-wave_real - DAMPING * wave_imag) + noise_wide[:, 1],
        ],
        1,
    ).astype(jnp.bfloat16)
    proj_columns = jnp.einsum(
        "zpxy,ny->zpnx", drive_term, mode_table, preferred_element_type=jnp.float32
    ).astype(jnp.bfloat16)
    block_part = lax.all_to_all(proj_columns, "my", split_axis=2, concat_axis=3, tiled=True)
    folded = jnp.einsum(
        "zpax,slx->zpsal", block_part, tiled_table, preferred_element_type=jnp.float32
    ).astype(jnp.bfloat16)
    proj_rows = folded.reshape(
        block_part.shape[0], block_part.shape[1], row_count * col_block * row_block
    )
    gathered_rows = lax.all_to_all(proj_rows, "mx", split_axis=2, concat_axis=0, tiled=True)
    slab_back = lax.dynamic_slice_in_dim(mode_table, rep_index * own_block, own_block, 0)[
        :, slab_first : slab_first + planes_all
    ]
    portion = lax.all_gather(gathered_rows, "rep", axis=0, tiled=True)
    plane_grid = portion.reshape(portion.shape[0], 2, col_block, row_block)
    summed = jnp.einsum("zpba,nz->pabn", plane_grid, slab_back, preferred_element_type=jnp.float32)
    return summed.astype(jnp.bfloat16)


def solution(mesh):
    in_specs = (P(None, "mx", "my", None), P(("rep", "mx"), None, "my", None), P())
    out_specs = P(None, "mx", "my", "rep")
    return jax.shard_map(body, mesh=mesh, in_specs=in_specs, out_specs=out_specs, check_vma=False)
```

profile of v0, /device:TPU:0, one launch (start us, length us, event | category | flops | bytes accessed | tf_op | source)
XLA Modules:
  0.0 974.2 jit_solution(4171945368356783076)
XLA Ops:
  7.8 25.5 %convert_bitcast_fusion.3 = bf16[32,2,96,192]{2,0,3,1:T(8,128)(2,1)} fusion(bf16[2,192,96,384]{3,2,1,0:T(8,128)(2,1)} %param.3, bf16[384,1536]{1,0:T(8,128)(2,1)S(1)} %copy-done, s32[]{:T(128)S(6)} %select_n.10), kind=kOutput, calls=%fused_computation.17 | convolution fusion | flops 907149312 | bytes 30769156 | tf_op jit(solution)/shard_map/pabk,kz->zpba/dot_general | solution.py:28
  33.3 5.1 copy.45
  38.5 6.9 reshape.28
  45.3 31.8 %all_to_all.51 = bf16[32,2,18432]{2,1,0:T(2,128)(2,1)S(1)} all-to-all(bf16[32,2,18432]{2,1,0:T(2,128)(2,1)S(1)} %reshape.28), channel_id=1, replica_groups=mesh['rep'=4,'mx'=2,'my'=4] {'mx'}, dimensions={0} | all-to-all | bytes 4718592 | tf_op jit(solution)/shard_map/all_to_all | solution.py:32
  84.2 37.8 %convert_element_type.34 = f32[16,2,384,1536]{3,2,1,0:T(8,128)} convert(bf16[16,2,384,1536]{3,2,1,0:T(8,128)(2,1)} %param.4) | non-fusion elementwise | flops 18874368 | bytes 113246208 | tf_op jit(solution)/shard_map/convert_element_type | solution.py:48
  122.1 180.8 %all-gather.3.cloned.1.call-done = bf16[16,2,2,384,192]{4,3,2,1,0:T(8,128)(2,1)} async-done(((bf16[16,2,2,96,192]{4,3,2,1,0:T(8,128)(2,1)}), bf16[16,2,2,384,192]{4,3,2,1,0:T(8,128)(2,1)}) %all-gather.3.cloned.1.call-update) | async-done | bytes 9437200 | tf_op jit(solution)/shard_map/all_gather | solution.py:38
  302.9 36.1 %fusion.6 = f32[16,2,384,1536]{3,2,1,0:T(8,128)} fusion(bf16[16,2,2,384,192]{4,3,2,1,0:T(8,128)(2,1)} %all-gather.3.cloned.1.call-done, bf16[384,1536]{1,0:T(8,128)(2,1)S(1)} %copy-done, bf16[2,192,1536]{2,1,0:T(8,128)(2,1)S(1)} %bitcast.69, s32[]{:T(128)S(6)} %select_n.11), kind=kOutput, calls=%fused_computation.10 | convolution fusion | flops 18124111872 | bytes 86409216 | tf_op jit(solution)/shard_map/zpax,ay->zpxy/dot_general | solution.py:42
  339.0 61.5 %fusion.1 = (bf16[16,1,384,1536]{3,2,1,0:T(8,128)(2,1)}, bf16[16,1,384,1536]{3,2,1,0:T(8,128)(2,1)}) fusion(f32[16,2,384,1536]{3,2,1,0:T(8,128)} %convert_element_type.34, f32[16,2,384,1536]{3,2,1,0:T(8,128)} %fusion.6), kind=kLoop, calls=%fused_computation.3 | loop fusion | flops 132120576 | bytes 188743680 | tf_op jit(solution)/shard_map/convert
  400.5 26.7 %convert_bitcast_fusion.1 = bf16[16,2,384,384]{2,3,1,0:T(8,128)(2,1)} fusion(bf16[16,1,384,1536]{3,2,1,0:T(8,128)(2,1)} %get-tuple-element.6, bf16[16,1,384,1536]{3,2,1,0:T(8,128)(2,1)} %get-tuple-element.5, bf16[384,1536]{1,0:T(8,128)(2,1)S(1)} %copy-done), kind=kOutput, calls=%fused_computation.15 | convolution fusion | flops 14519107584 | bytes 48365568 | tf_op jit(solution)/shard_map/zpxy,ny->zpnx/dot_general | solution.py:56
  427.2 23.9 %copy.29 = bf16[16,2,384,384]{3,1,0,2:T(2,128)(2,1)} copy(bf16[16,2,384,384]{2,3,1,0:T(8,128)(2,1)} %convert_bitcast_fusion.1) | data formatting | bytes 18874368 | tf_op jit(solution)/shard_map/convert_element_type | solution.py:58
  451.1 214.1 %all_to_all.52 = bf16[16,2,384,384]{3,1,0,2:T(2,128)(2,1)} all-to-all(bf16[16,2,384,384]{3,1,0,2:T(2,128)(2,1)} %copy.29), channel_id=1, replica_groups=mesh['rep'=4,'mx'=2,'my'=4] {'my'}, dimensions={2} | all-to-all | bytes 18874368 | tf_op jit(solution)/shard_map/all_to_all | solution.py:59
  665.3 10.9 %copy.30 = bf16[16,2,384,384]{3,2,1,0:T(8,128)(2,1)} copy(bf16[16,2,384,384]{3,1,0,2:T(2,128)(2,1)} %all_to_all.52) | data formatting | bytes 18874368 | tf_op jit(solution)/shard_map/all_to_all | solution.py:59
  676.2 10.6 %copy.31 = bf16[16,2,96,4,384]{4,3,2,1,0:T(4,128)(2,1)} copy(bf16[16,2,96,4,384]{4,2,3,1,0:T(8,128)(2,1)} %bitcast.73) | data formatting | bytes 18874368 | tf_op jit(solution)/shard_map/all_to_all | solution.py:59
  686.8 15.9 %reshape.25 = bf16[16,2,96,1536,1]{3,2,1,0,4:T(8,128)(2,1)} reshape(bf16[16,2,96,4,384]{4,3,2,1,0:T(4,128)(2,1)} %copy.31) | data formatting | bytes 18874368 | tf_op jit(solution)/shard_map/all_to_all | solution.py:59
  702.7 10.2 %convert_bitcast_fusion.2 = bf16[16,2,2,96,192]{4,3,2,1,0:T(8,128)(2,1)} fusion(bf16[2,192,1536,1,1]{2,1,0,4,3:T(8,128)(2,1)S(1)} %bitcast.68, bf16[16,2,96,1536,1]{3,2,1,0,4:T(8,128)(2,1)} %reshape.25), kind=kOutput, calls=%fused_computation.16 | convolution fusion | flops 3625058304 | bytes 12976128 | tf_op jit(solution)/shard_map/zpax,slx->zpsal/dot_general | solution.py:60
  712.8 35.2 %copy.46 = bf16[16,2,2,96,192]{0,1,4,3,2:T(2,128)(2,1)} copy(bf16[16,2,2,96,192]{4,3,2,1,0:T(8,128)(2,1)} %convert_bitcast_fusion.2) | data formatting | bytes 4718592 | tf_op jit(solution)/shard_map/reshape | solution.py:63
  748.1 27.3 %reshape.30 = bf16[2,2,294912]{2,1,0:T(2,128)(2,1)S(1)} reshape(bf16[36864,2,16]{2,1,0:T(2,128)(2,1)} %bitcast.70) | data formatting | bytes 4718592
  775.3 30.9 %all_to_all.53 = bf16[2,2,294912]{2,1,0:T(2,128)(2,1)} all-to-all(bf16[2,2,294912]{2,1,0:T(2,128)(2,1)S(1)} %reshape.30), channel_id=1, replica_groups=mesh['rep'=4,'mx'=2,'my'=4] {'mx'}, dimensions={0} | all-to-all | bytes 4718592 | tf_op jit(solution)/shard_map/all_to_all | solution.py:66
  806.2 22.4 %reshape.31 = bf16[36864,2,16]{2,1,0:T(2,128)(2,1)} reshape(bf16[2,2,294912]{2,1,0:T(2,128)(2,1)} %all_to_all.53) | data formatting | bytes 4718592
  828.6 35.6 %copy.34 = bf16[2,16,2,18432]{3,1,0,2:T(8,128)(2,1)} copy(bf16[2,16,2,18432]{1,2,3,0:T(2,128)(2,1)} %bitcast.71) | data formatting | bytes 4718592 | tf_op jit(solution)/shard_map/all_to_all | solution.py:66
  864.2 62.8 %all-gather.5.cloned.1.call-done = bf16[128,2,18432]{2,0,1:T(8,128)(2,1)} async-done(((bf16[32,2,18432]{2,0,1:T(8,128)(2,1)}), bf16[128,2,18432]{2,0,1:T(8,128)(2,1)}) %all-gather.5.cloned.1.call-update) | async-done | bytes 9437200 | tf_op jit(solution)/shard_map/all_gather | solution.py:70
  927.0 12.6 %copy.35 = bf16[128,2,18432]{0,2,1:T(8,128)(2,1)} copy(bf16[128,2,18432]{2,0,1:T(8,128)(2,1)} %all-gather.5.cloned.1.call-done) | data formatting | bytes 18874368 | tf_op jit(solution)/shard_map/all_gather | solution.py:70
  939.6 13.8 %convert_bitcast_fusion = bf16[2,192,96,96]{1,3,2,0:T(8,128)(2,1)} fusion(bf16[128,2,96,192]{0,3,2,1:T(8,128)(2,1)} %bitcast.72, bf16[384,1536]{1,0:T(8,128)(2,1)S(1)} %copy-done, s32[]{:T(128)S(6)} %select_n.9, s32[]{:T(128)S(6)} %add.30), kind=kOutput, calls=%fused_computation.14 | convolution fusion | flops 909508608 | bytes 16539656 | tf_op jit(solution)/shard_map/zpba,nz->pabn/dot_general | solution.py:72
  953.3 13.9 %copy.36 = bf16[2,192,96,96]{3,2,1,0:T(8,128)(2,1)} copy(bf16[2,192,96,96]{1,3,2,0:T(8,128)(2,1)} %convert_bitcast_fusion) | data formatting | bytes 14155776 | tf_op jit(solution)/shard_map/convert_element_type | solution.py:73
  (8 shorter events, 8.4 us)
Async XLA Ops:
  6.5 1.3 copy-start
  6.5 296.3 %all-gather.3.cloned.1.call-start = ((), (), s32[]{:S(2)}) async-start(), calls=%async_computation.3 | async-start | bytes 15728640 | tf_op jit(solution)/shard_map/all_gather | solution.py:38
  84.0 843.0 %all-gather.5.cloned.1.call-start = ((), (), s32[]{:S(2)}) async-start(), calls=%async_computation.4 | async-start | bytes 11796480 | tf_op jit(solution)/shard_map/all_gather | solution.py:70
Sparse Core Ops, SparseCore 0:
  84.1 218.6 all-gather.2
  864.3 62.6 all-gather.4
where the time goes:
time: 986 us; the launch traced here: 974 us
  blocking collectives  277 us (28%)
  waiting for transfers between devices  244 us (25%)
  local copies, waits for them, and re-layouts  228 us (23%)
  matrix products  112 us (11%)
  other arithmetic  99.4 us (10%)
  between operations  13.6 us (1%)
    all_to_all x1, blocking collectives, body(): lax.all_to_all(proj_columns, 'my', split_axis=2, concat_axis=3, tiled=True)  214 us
    all_gather x1, waiting for transfers between devices, body(): lax.all_gather(grouped, 'my', axis=3, tiled=True)  181 us
    all_gather x1, waiting for transfers between devices, body(): portion = lax.all_gather(gathered_rows, 'rep', axis=0, tiled=True)  62.8 us
    another operation x1, other arithmetic  61.5 us
    unnamed x4, local copies, waits for them, and re-layouts  50.9 us
    convert_element_type x1, other arithmetic, body(): noise_wide = noise_field.astype(jnp.float32)  37.8 us
    all_to_all x3, local copies, waits for them, and re-layouts, body(): lax.all_to_all(proj_columns, 'my', split_axis=2, concat_axis=3, tiled=True)  37.4 us
    dot_general x1, matrix products, body(): jnp.einsum('zpax,ay->zpxy', block_part, mode_table, preferred_element_typ...  36.1 us
  transfers between devices with their start and end apart: 2, of which 2 were waited for; matrix products, arithmetic and copies ran while one was open for 4% of the time, Pallas kernels for 0%

commit v1 on v0

--- a/solution.py
+++ b/solution.py
@@ -56,7 +56,10 @@
     proj_columns = jnp.einsum(
         "zpxy,ny->zpnx", drive_term, mode_table, preferred_element_type=jnp.float32
     ).astype(jnp.bfloat16)
-    block_part = lax.all_to_all(proj_columns, "my", split_axis=2, concat_axis=3, tiled=True)
+    block_part = jnp.concatenate(
+        lax.all_to_all(jnp.stack(jnp.split(proj_columns, lax.axis_size("my"), axis=2)), "my", 0, 0),
+        axis=3,
+    )
     folded = jnp.einsum(
         "zpax,slx->zpsal", block_part, tiled_table, preferred_element_type=jnp.float32
     ).astype(jnp.bfloat16)

time: 986 us -> 947 us (0.960)
  local copies, waits for them, and re-layouts: 228 us -> 201 us
    all_to_all x3 -> x0, local copies, waits for them, and re-layouts: 37.4 us -> none  [body(): lax.all_to_all(proj_columns, 'my', split_axis=2, concat_axis=3, tiled=True)]
    reshape x0 -> x2, local copies, waits for them, and re-layouts: none -> 32.2 us  [body(): jnp.concatenate(lax.all_to_all(jnp.stack(jnp.split(proj_columns, lax.axis...]
    convert_element_type x1 -> x0, local copies, waits for them, and re-layouts: 23.9 us -> none  [body(): proj_columns = jnp.einsum('zpxy,ny->zpnx', drive_term, mode_table, prefer...]
    another operation x1 -> x2, other arithmetic: 61.5 us -> 62.9 us
where the time goes in v1:
time: 947 us; the launch traced here: 935 us
  blocking collectives  271 us (29%)
  waiting for transfers between devices  244 us (26%)
  local copies, waits for them, and re-layouts  201 us (21%)
  matrix products  105 us (11%)
  other arithmetic  101 us (11%)
  between operations  13.6 us (1%)
    all_to_all x1, blocking collectives, body(): lax.all_to_all(jnp.stack(jnp.split(proj_columns, lax.axis_size('my'), axi...  209 us
    all_gather x1, waiting for transfers between devices, body(): lax.all_gather(grouped, 'my', axis=3, tiled=True)  181 us
    all_gather x1, waiting for transfers between devices, body(): portion = lax.all_gather(gathered_rows, 'rep', axis=0, tiled=True)  62.8 us
    another operation x1, other arithmetic  61.4 us
    unnamed x4, local copies, waits for them, and re-layouts  50.9 us
    convert_element_type x1, other arithmetic, body(): noise_wide = noise_field.astype(jnp.float32)  37.8 us
    dot_general x1, matrix products, body(): jnp.einsum('zpax,ay->zpxy', block_part, mode_table, preferred_element_typ...  36.1 us
    all_to_all x1, local copies, waits for them, and re-layouts, body(): lax.all_to_all(proj_rows, 'mx', split_axis=2, concat_axis=0, tiled=True)  35.6 us
  transfers between devices with their start and end apart: 2, of which 2 were waited for; matrix products, arithmetic and copies ran while one was open for 4% of the time, Pallas kernels for 0%

profile of v1, /device:TPU:0, one launch (start us, length us, event | category | flops | bytes accessed | tf_op | source)
XLA Modules:
  0.0 935.4 jit_solution(10832351998650225365)
XLA Ops:
  7.8 25.5 %convert_bitcast_fusion.3 = bf16[32,2,96,192]{2,0,3,1:T(8,128)(2,1)} fusion(bf16[2,192,96,384]{3,2,1,0:T(8,128)(2,1)} %param.3, bf16[384,1536]{1,0:T(8,128)(2,1)S(1)} %copy-done, s32[]{:T(128)S(6)} %select_n.10), kind=kOutput, calls=%fused_computation.18 | convolution fusion | flops 907149312 | bytes 30769156 | tf_op jit(solution)/shard_map/pabk,kz->zpba/dot_general | solution.py:28
  33.3 5.1 copy.40
  38.5 6.9 reshape.36
  45.3 31.8 %all_to_all.38 = bf16[32,2,18432]{2,1,0:T(2,128)(2,1)S(1)} all-to-all(bf16[32,2,18432]{2,1,0:T(2,128)(2,1)S(1)} %reshape.36), channel_id=1, replica_groups=mesh['rep'=4,'mx'=2,'my'=4] {'mx'}, dimensions={0} | all-to-all | bytes 4718592 | tf_op jit(solution)/shard_map/all_to_all | solution.py:32
  77.1 2.4 copy.47
  79.5 4.5 reshape.23
  84.2 37.8 %convert_element_type.34 = f32[16,2,384,1536]{3,2,1,0:T(8,128)} convert(bf16[16,2,384,1536]{3,2,1,0:T(8,128)(2,1)} %param.4) | non-fusion elementwise | flops 18874368 | bytes 113246208 | tf_op jit(solution)/shard_map/convert_element_type | solution.py:48
  122.1 180.8 %all-gather.3.cloned.1.call-done = bf16[16,2,2,384,192]{4,3,2,1,0:T(8,128)(2,1)} async-done(((bf16[16,2,2,96,192]{4,3,2,1,0:T(8,128)(2,1)}), bf16[16,2,2,384,192]{4,3,2,1,0:T(8,128)(2,1)}) %all-gather.3.cloned.1.call-update) | async-done | bytes 9437200 | tf_op jit(solution)/shard_map/all_gather | solution.py:38
  302.9 36.1 %fusion.6 = f32[16,2,384,1536]{3,2,1,0:T(8,128)} fusion(bf16[16,2,2,384,192]{4,3,2,1,0:T(8,128)(2,1)} %all-gather.3.cloned.1.call-done, bf16[384,1536]{1,0:T(8,128)(2,1)S(1)} %copy-done, bf16[2,192,1536]{2,1,0:T(8,128)(2,1)S(1)} %bitcast.75, s32[]{:T(128)S(6)} %select_n.11), kind=kOutput, calls=%fused_computation.10 | convolution fusion | flops 18124111872 | bytes 86409216 | tf_op jit(solution)/shard_map/zpax,ay->zpxy/dot_general | solution.py:42
  339.0 61.4 %fusion.1 = (bf16[16,1,384,1536]{3,2,1,0:T(8,128)(2,1)}, bf16[16,1,384,1536]{3,2,1,0:T(8,128)(2,1)}) fusion(f32[16,2,384,1536]{3,2,1,0:T(8,128)} %convert_element_type.34, f32[16,2,384,1536]{3,2,1,0:T(8,128)} %fusion.6), kind=kLoop, calls=%fused_computation.3 | loop fusion | flops 132120576 | bytes 188743680 | tf_op jit(solution)/shard_map/convert
  400.4 19.5 %convert_bitcast_fusion.1 = bf16[16,2,384,384]{3,2,1,0:T(8,128)(2,1)S(1)} fusion(bf16[16,1,384,1536]{3,2,1,0:T(8,128)(2,1)} %get-tuple-element.6, bf16[16,1,384,1536]{3,2,1,0:T(8,128)(2,1)} %get-tuple-element.5, bf16[384,1536]{1,0:T(8,128)(2,1)S(1)} %copy-done), kind=kOutput, calls=%fused_computation.16 | convolution fusion | flops 14519107584 | bytes 48365568 | tf_op jit(solution)/shard_map/zpxy,ny->zpnx/dot_general | solution.py:56
  422.8 208.7 %all_to_all.39 = bf16[4,16,2,96,384]{4,3,2,1,0:T(8,128)(2,1)S(1)} all-to-all(bf16[4,16,2,96,384]{4,3,2,1,0:T(8,128)(2,1)S(1)} %pad_maximum_fusion), channel_id=1, replica_groups=mesh['rep'=4,'mx'=2,'my'=4] {'my'}, dimensions={0} | all-to-all | bytes 18874368 | tf_op jit(solution)/shard_map/all_to_all | solution.py:60
  631.5 16.2 %copy.26 = bf16[16,2,96,4,384]{4,3,2,1,0:T(4,128)(2,1)} copy(bf16[16,2,96,4,384]{4,2,1,0,3:T(8,128)(2,1)S(1)} %bitcast.79) | data formatting | bytes 18874368 | tf_op jit(solution)/shard_map/reshape | solution.py:59
  647.8 15.9 %reshape.33 = bf16[16,2,96,1536,1]{3,2,1,0,4:T(8,128)(2,1)} reshape(bf16[16,2,96,4,384]{4,3,2,1,0:T(4,128)(2,1)} %copy.26) | data formatting | bytes 18874368 | tf_op jit(solution)/shard_map/reshape | solution.py:59
  663.7 10.1 %convert_bitcast_fusion.2 = bf16[16,2,2,96,192]{4,3,2,1,0:T(8,128)(2,1)} fusion(bf16[2,192,1536,1,1]{2,1,0,4,3:T(8,128)(2,1)S(1)} %bitcast.74, bf16[16,2,96,1536,1]{3,2,1,0,4:T(8,128)(2,1)} %reshape.33), kind=kOutput, calls=%fused_computation.17 | convolution fusion | flops 3625058304 | bytes 12976128 | tf_op jit(solution)/shard_map/zpax,slx->zpsal/dot_general | solution.py:63
  673.8 35.4 %copy.41 = bf16[16,2,2,96,192]{0,1,4,3,2:T(2,128)(2,1)} copy(bf16[16,2,2,96,192]{4,3,2,1,0:T(8,128)(2,1)} %convert_bitcast_fusion.2) | data formatting | bytes 4718592 | tf_op jit(solution)/shard_map/reshape | solution.py:66
  709.3 27.2 %reshape.38 = bf16[2,2,294912]{2,1,0:T(2,128)(2,1)S(1)} reshape(bf16[36864,2,16]{2,1,0:T(2,128)(2,1)} %bitcast.76) | data formatting | bytes 4718592
  736.5 30.9 %all_to_all.40 = bf16[2,2,294912]{2,1,0:T(2,128)(2,1)} all-to-all(bf16[2,2,294912]{2,1,0:T(2,128)(2,1)S(1)} %reshape.38), channel_id=1, replica_groups=mesh['rep'=4,'mx'=2,'my'=4] {'mx'}, dimensions={0} | all-to-all | bytes 4718592 | tf_op jit(solution)/shard_map/all_to_all | solution.py:69
  767.3 22.4 %reshape.39 = bf16[36864,2,16]{2,1,0:T(2,128)(2,1)} reshape(bf16[2,2,294912]{2,1,0:T(2,128)(2,1)} %all_to_all.40) | data formatting | bytes 4718592
  789.7 35.6 %copy.29 = bf16[2,16,2,18432]{3,1,0,2:T(8,128)(2,1)} copy(bf16[2,16,2,18432]{1,2,3,0:T(2,128)(2,1)} %bitcast.77) | data formatting | bytes 4718592 | tf_op jit(solution)/shard_map/all_to_all | solution.py:69
  825.3 62.8 %all-gather.5.cloned.1.call-done = bf16[128,2,18432]{2,0,1:T(8,128)(2,1)} async-done(((bf16[32,2,18432]{2,0,1:T(8,128)(2,1)}), bf16[128,2,18432]{2,0,1:T(8,128)(2,1)}) %all-gather.5.cloned.1.call-update) | async-done | bytes 9437200 | tf_op jit(solution)/shard_map/all_gather | solution.py:73
  888.1 12.6 %copy.30 = bf16[128,2,18432]{0,2,1:T(8,128)(2,1)} copy(bf16[128,2,18432]{2,0,1:T(8,128)(2,1)} %all-gather.5.cloned.1.call-done) | data formatting | bytes 18874368 | tf_op jit(solution)/shard_map/all_gather | solution.py:73
  900.7 13.8 %convert_bitcast_fusion = bf16[2,192,96,96]{1,3,2,0:T(8,128)(2,1)} fusion(bf16[128,2,96,192]{0,3,2,1:T(8,128)(2,1)} %bitcast.78, bf16[384,1536]{1,0:T(8,128)(2,1)S(1)} %copy-done, s32[]{:T(128)S(6)} %select_n.9, s32[]{:T(128)S(6)} %add.30), kind=kOutput, calls=%fused_computation.15 | convolution fusion | flops 909508608 | bytes 16539656 | tf_op jit(solution)/shard_map/zpba,nz->pabn/dot_general | solution.py:75
  914.5 13.9 %copy.31 = bf16[2,192,96,96]{3,2,1,0:T(8,128)(2,1)} copy(bf16[2,192,96,96]{1,3,2,0:T(8,128)(2,1)} %convert_bitcast_fusion) | data formatting | bytes 14155776 | tf_op jit(solution)/shard_map/convert_element_type | solution.py:76
  (8 shorter events, 4.5 us)
Async XLA Ops:
  6.5 1.3 copy-start
  6.5 296.3 %all-gather.3.cloned.1.call-start = ((), (), s32[]{:S(2)}) async-start(), calls=%async_computation.3 | async-start | bytes 15728640 | tf_op jit(solution)/shard_map/all_gather | solution.py:38
  84.0 804.1 %all-gather.5.cloned.1.call-start = ((), (), s32[]{:S(2)}) async-start(), calls=%async_computation.4 | async-start | bytes 11796480 | tf_op jit(solution)/shard_map/all_gather | solution.py:73
Sparse Core Ops, SparseCore 0:
  84.1 218.6 all-gather.2
  825.5 62.6 all-gather.4
